TPU v7x, 128 devices: a whole 4x4x4 slice. The times are simulated.
128 devices in a mesh: tok: 16 (over x, y_lo, core), col: 8 (over y_hi, z).
Axes of the slice: x: 4, y: 4 (y_hi: 2, y_lo: 2; y = y_hi * 2 + y_lo), z: 4, core: 2. Of those that a mesh axis runs over, the one named last changes fastest.
Arguments:
- activations: bfloat16 [2, 24576, 4096], P(None, 'tok', 'col'), may hold values from -6 to 6
- out_grads: bfloat16 [2, 24576, 4096], P(None, 'tok', 'col'), may hold values from -0.059814453 to 0.059814453
- token_mask: int32 [2, 24576], P(None, 'tok'), may hold values 0 or 1
- row_signs: int32 [4096], P('tok'), may hold values from 0 to 1
- col_signs: int32 [4096], P('col'), may hold values from 0 to 1
- bank: float32 [16, 4096, 4096], P(None, 'tok', 'col'), may hold values from -6 to 6
- bank_index: int32 [2], replicated, may hold values from 0 to 15, as said below
Outputs:
- fingerprints: float32 [2, 4096, 4096], P(None, 'tok', 'col')
- scores: float32 [2], replicated
Inputs may be any that keep to these rules, and one draw needn't show every extreme that they name: `bank_index`: the 2 values are distinct, and one of them is 15.
All inputs are finite; a program needn't handle non-finite values. No bound on the sum of `token_mask` on one device may be relied on, other than what follows from the above.
Results may differ from a plain program's by a relative error of at most 0.0003.
Values may be sent and summed in bfloat16 or wider, within the bound.
A program may use at most 128 MiB of HBM per device.

v0:
```python
import functools
import math
import jax
import jax.numpy as jnp
from jax import lax
from jax.sharding import Mesh
from jax.sharding import PartitionSpec as P

D = 4096
TOK = ("tok_0", "tok_1", "tok_2")
COL = ("col_0", "col_1")
TOK_COL = ("tok_0", "tok_1", "tok_2", "col_0", "col_1")
HIGH = lax.Precision.HIGHEST


def copy_for_each(x, axis):
    peers = lax.axis_size(axis)
    return lax.all_to_all(jnp.broadcast_to(x[None], (peers, *x.shape)), axis, 0, 0, tiled=True)


def joined_along(pieces, dim):
    lengths = list(pieces.shape[1:])
    lengths[dim] *= pieces.shape[0]
    return jnp.moveaxis(pieces, 0, dim).reshape(lengths)


def gathered_copies(x, axis, dim):
    pieces = copy_for_each(x, axis)
    return joined_along(pieces, dim)


def one_axis_at_a_time(x, axes):
    return functools.reduce(lax.psum, axes, x)


def hadamard(order):
    positions = jnp.arange(order, dtype=jnp.int32)
    common_bits = jnp.bitwise_and(positions[:, None], positions[None, :])
    parity = jnp.zeros((order, order), jnp.int32)
    for bit_number in range(max(order.bit_length() - 1, 0)):
        parity = parity + jnp.bitwise_and(jnp.right_shift(common_bits, bit_number), 1)
    return (1 - 2 * (parity % 2)).astype(jnp.float32)


def body(activations, out_grads, token_mask, row_signs, col_signs, bank, bank_index):
    row_pm = (2 * row_signs - 1).astype(jnp.float32)
    col_pm = (2 * col_signs - 1).astype(jnp.float32)
    tok_count = lax.axis_size(TOK)
    col_count = lax.axis_size(COL)
    local_rows = row_pm.shape[0]
    local_cols = col_pm.shape[0]
    tok_table = hadamard(tok_count)
    col_table = hadamard(col_count)
    rows_table = hadamard(local_rows)
    cols_table = hadamard(local_cols)
    factor = 1.0 / math.sqrt(D)
    squared = float(D) * float(D)
    all_signs = gathered_copies(row_signs, TOK, 0)
    full_pm = (2 * all_signs - 1).astype(jnp.float32)
    prints = []
    crosses = []
    owns = []
    refsqs = []
    for seq_number in range(activations.shape[0]):
        features = lax.all_gather(activations[seq_number], COL, axis=1, tiled=True)
        masked = out_grads[seq_number] * token_mask[seq_number][:, None].astype(jnp.bfloat16)
        partial_value = jnp.einsum(
            "tr,tc->rc", features, masked, preferred_element_type=jnp.float32
        )
        blocks = (partial_value * full_pm[:, None]).reshape(tok_count, local_rows, local_cols)
        blocks = jnp.einsum("rs,asc->arc", rows_table, blocks, precision=HIGH)
        blocks = jnp.einsum("ab,brc->arc", tok_table, blocks, precision=HIGH)
        premixed = blocks.reshape(tok_count * local_rows, local_cols)

        def term_rows(row_start, row_count, premixed=premixed):
            return premixed

        summed = lax.psum_scatter(
            term_rows(jnp.int32(0), lax.axis_size(TOK) * local_rows),
            TOK,
            scatter_dimension=0,
            tiled=True,
        )
        slab = summed
        slab = slab * factor
        slab = jnp.dot(slab * col_pm[None, :], cols_table, precision=HIGH)
        pieces = slab.reshape(col_count, local_rows // col_count, local_cols)
        col_pieces = lax.all_to_all(pieces, COL, split_axis=0, concat_axis=0, tiled=True)
        mixed_cols = jnp.einsum("ab,brc->arc", col_table, col_pieces, precision=HIGH)
        pieces = lax.all_to_all(mixed_cols, COL, split_axis=0, concat_axis=0, tiled=True)
        slab = pieces.reshape(local_rows, local_cols)
        slab = slab * factor
        chosen = lax.dynamic_index_in_dim(bank, bank_index[seq_number], 0, keepdims=False)
        prints.append(slab)
        crosses.append(jnp.sum(slab * chosen))
        owns.append(jnp.sum(slab * slab))
        refsqs.append(jnp.sum(chosen * chosen))
    cross, own, refsq = (
        one_axis_at_a_time(jnp.stack(crosses), TOK_COL),
        one_axis_at_a_time(jnp.stack(owns), TOK_COL),
        one_axis_at_a_time(jnp.stack(refsqs), TOK_COL),
    )
    scores = D * (cross / squared) / jnp.sqrt((own / squared + 1e-06) * (refsq / squared + 1e-06))
    return (jnp.stack(prints), scores)


def solution(mesh):
    split = Mesh(mesh.devices.reshape(4, 2, 2, 2, 4), ("tok_0", "tok_1", "tok_2", "col_0", "col_1"))
    return jax.shard_map(
        body,
        mesh=split,
        in_specs=(
            P(None, TOK, COL),
            P(None, TOK, COL),
            P(None, TOK),
            P(TOK),
            P(COL),
            P(None, TOK, COL),
            P(),
        ),
        out_specs=(P(None, TOK, COL), P()),
        check_vma=False,
    )
```

profile of v0, /device:TPU:0, one launch (start us, length us, event | category | flops | bytes accessed | tf_op | source)
XLA Modules:
  0.0 617.7 jit_solution(9460281022073052252)
XLA Ops:
  12.6 5.5 all-to-all-start
  18.3 6.0 all-to-all-done
  24.3 142.2 %all-gather.7.cloned.1.call-done = bf16[1,1536,4096]{2,1,0:T(8,128)(2,1)} async-done(((bf16[1,1536,512]{2,1,0:T(8,128)(2,1)}), bf16[1,1536,4096]{2,1,0:T(8,128)(2,1)}) %all-gather.7.cloned.1.call-update) | async-done | bytes 12582928 | tf_op jit(solution)/shard_map/all_gather | solution.py:65
  166.5 10.4 %fusion.7 = f32[512,4096]{1,0:T(8,128)S(1)} fusion(bf16[1,1536,4096]{2,1,0:T(8,128)(2,1)} %all-gather.7.cloned.1.call-done, f32[4096]{0:T(1024)S(1)} %bitcast.87, bf16[2,1536,512]{2,1,0:T(8,128)(2,1)S(1)} %copy-done.4, bf16[1536]{0:T(1024)(128)(2,1)S(1)} %get-tuple-element.7), kind=kOutput, calls=%fused_computation.5 | convolution fusion | flops 6445334528 | bytes 22564864 | tf_op jit(solution)/shard_map/tr,tc->rc/dot_general | solution.py:67
  180.8 9.6 %convolution_bitcast_fusion = f32[16,256,512]{1,0,2:T(8,128)} fusion(f32[16,256,512]{1,0,2:T(8,128)S(1)} %bitcast.81), kind=kOutput, calls=%fused_computation.6 | convolution fusion | flops 6444941312 | bytes 16777216 | tf_op jit(solution)/shard_map/rs,asc->arc/dot_general | solution.py:71
  190.4 10.5 %copy.23 = f32[16,256,512]{2,0,1:T(8,128)} copy(f32[16,256,512]{1,0,2:T(8,128)} %convolution_bitcast_fusion) | data formatting | bytes 16777216 | tf_op jit(solution)/shard_map/rs,asc->arc/transpose | solution.py:71
  200.9 11.6 %fusion.62 = f32[16,256,512]{2,0,1:T(8,128)S(1)} fusion(f32[16,256,512]{2,0,1:T(8,128)} %copy.23), kind=kOutput, calls=%fused_computation.77 | convolution fusion | flops 402659840 | bytes 16777216 | tf_op jit(solution)/shard_map/ab,brc->arc/dot_general | solution.py:72
  212.5 8.0 %copy.24 = f32[16,256,512]{2,1,0:T(8,128)} copy(f32[16,256,512]{2,0,1:T(8,128)S(1)} %fusion.62) | data formatting | bytes 16777216 | tf_op jit(solution)/shard_map/ab,brc->arc/dot_general | solution.py:72
  220.6 98.5 %all-gather.5.cloned.1.call-done = bf16[1,1536,4096]{2,1,0:T(8,128)(2,1)} async-done(((bf16[1,1536,512]{2,1,0:T(8,128)(2,1)}), bf16[1,1536,4096]{2,1,0:T(8,128)(2,1)}) %all-gather.5.cloned.1.call-update) | async-done | bytes 12582928 | tf_op jit(solution)/shard_map/all_gather | solution.py:65
  319.1 10.6 %fusion.4 = f32[512,4096]{1,0:T(8,128)S(1)} fusion(bf16[1,1536,4096]{2,1,0:T(8,128)(2,1)} %all-gather.5.cloned.1.call-done, f32[4096]{0:T(1024)S(1)} %bitcast.88, bf16[2,1536,512]{2,1,0:T(8,128)(2,1)S(1)} %copy-done.4, bf16[1536]{0:T(1024)(128)(2,1)S(1)} %get-tuple-element.6), kind=kOutput, calls=%fused_computation.4 | convolution fusion | flops 6445334528 | bytes 22564864 | tf_op jit(solution)/shard_map/tr,tc->rc/dot_general | solution.py:67
  333.5 9.6 %convolution_bitcast_fusion.1 = f32[16,256,512]{1,0,2:T(8,128)} fusion(f32[16,256,512]{1,0,2:T(8,128)S(1)} %bitcast.82), kind=kOutput, calls=%fused_computation.7 | convolution fusion | flops 6444941312 | bytes 16777216 | tf_op jit(solution)/shard_map/rs,asc->arc/dot_general | solution.py:71
  343.2 10.5 %copy.19 = f32[16,256,512]{2,0,1:T(8,128)} copy(f32[16,256,512]{1,0,2:T(8,128)} %convolution_bitcast_fusion.1) | data formatting | bytes 16777216 | tf_op jit(solution)/shard_map/rs,asc->arc/transpose | solution.py:71
  353.7 11.8 %fusion.64 = f32[16,256,512]{2,0,1:T(8,128)S(1)} fusion(f32[16,256,512]{2,0,1:T(8,128)} %copy.19), kind=kOutput, calls=%fused_computation.78 | convolution fusion | flops 402659840 | bytes 16777216 | tf_op jit(solution)/shard_map/ab,brc->arc/dot_general | solution.py:72
  365.5 8.1 %copy.20 = f32[16,256,512]{2,1,0:T(8,128)} copy(f32[16,256,512]{2,0,1:T(8,128)S(1)} %fusion.64) | data formatting | bytes 16777216 | tf_op jit(solution)/shard_map/ab,brc->arc/dot_general | solution.py:72
  374.2 41.1 %reduce-scatter.5.cloned.1.call-done = f32[256,512]{1,0:T(8,128)} async-done(((f32[4096,512]{1,0:T(8,128)}), f32[256,512]{1,0:T(8,128)}) %reduce-scatter.5.cloned.1.call-update) | async-done | bytes 524304 | tf_op jit(solution)/shard_map/reduce_scatter | solution.py:78
  419.7 4.9 all-to-all-start.3
  424.6 92.7 %reduce-scatter.3.cloned.1.call-done = f32[256,512]{1,0:T(8,128)} async-done(((f32[4096,512]{1,0:T(8,128)}), f32[256,512]{1,0:T(8,128)}) %reduce-scatter.3.cloned.1.call-update) | async-done | bytes 524304 | tf_op jit(solution)/shard_map/reduce_scatter | solution.py:78
  521.6 7.2 %all-to-all-start.1 = ((f32[8,32,512]{2,1,0:T(8,128)}), f32[8,32,512]{2,1,0:T(8,128)S(1)}, u32[]{:S(2)}, u32[]{:S(2)}) async-start(f32[8,32,512]{2,1,0:T(8,128)} %bitcast.9), calls=%async_computation.2 | async-start | bytes 1048576 | tf_op jit(solution)/shard_map/all_to_all | solution.py:88
  530.7 9.4 %all-to-all-done.1 = f32[8,32,512]{2,1,0:T(8,128)S(1)} async-done(((f32[8,32,512]{2,1,0:T(8,128)}), f32[8,32,512]{2,1,0:T(8,128)S(1)}, u32[]{:S(2)}, u32[]{:S(2)}) %all-to-all-start.1) | async-done | bytes 524320 | tf_op jit(solution)/shard_map/all_to_all | solution.py:88
  546.4 9.3 %all-to-all-done.4 = f32[8,32,512]{2,1,0:T(8,128)S(1)} async-done(((f32[8,32,512]{2,1,0:T(8,128)}), f32[8,32,512]{2,1,0:T(8,128)S(1)}, u32[]{:S(2)}, u32[]{:S(2)}) %all-to-all-start.4) | async-done | bytes 524320 | tf_op jit(solution)/shard_map/all_to_all | solution.py:90
  564.4 5.8 all-to-all-done.2
  578.0 9.7 %all-reduce.1 = (f32[2]{0:T(128)S(1)}, f32[2]{0:T(128)S(1)}, f32[2]{0:T(128)S(1)}) all-reduce(f32[2]{0:T(128)S(1)} %pad_maximum_fusion.3, f32[2]{0:T(128)S(1)} %get-tuple-element.32, f32[2]{0:T(128)S(1)} %get-tuple-element.31), channel_id=1, replica_groups=mesh['tok_0'=4,'tok_1'=2,'tok_2'=2,'col_0'=2,'col_1'=4] {'tok_0'}, use_global_device_ids=true, to_apply=%region_18.19 | all-reduce | flops 6 | bytes 48 | tf_op jit(solution)/shard_map/psum | solution.py:33
  595.1 6.4 %all-reduce.2 = (f32[2]{0:T(128)S(1)}, f32[2]{0:T(128)S(1)}, f32[2]{0:T(128)S(1)}) all-reduce(f32[2]{0:T(128)S(1)} %get-tuple-element.17, f32[2]{0:T(128)S(1)} %get-tuple-element.18, f32[2]{0:T(128)S(1)} %get-tuple-element.19), channel_id=1, replica_groups=mesh['tok_0'=4,'tok_1'=2,'tok_2'=2,'col_0'=2,'col_1'=4] {'col_0'}, use_global_device_ids=true, to_apply=%region_21.22 | all-reduce | flops 6 | bytes 48 | tf_op jit(solution)/shard_map/psum | solution.py:33
  601.5 9.0 %all-reduce = (f32[2]{0:T(128)S(1)}, f32[2]{0:T(128)S(1)}, f32[2]{0:T(128)S(1)}) all-reduce(f32[2]{0:T(128)S(1)} %get-tuple-element.14, f32[2]{0:T(128)S(1)} %get-tuple-element.15, f32[2]{0:T(128)S(1)} %get-tuple-element.16), channel_id=1, replica_groups=mesh['tok_0'=4,'tok_1'=2,'tok_2'=2,'col_0'=2,'col_1'=4] {'col_1'}, use_global_device_ids=true, to_apply=%region_22.23 | all-reduce | flops 6 | bytes 48 | tf_op jit(solution)/shard_map/psum | solution.py:33
  (45 shorter events, 51.3 us)
Async XLA Ops:
  7.2 4.8 copy-start.3
  7.2 11.0 %copy-start = (s32[2,1536]{1,0:T(2,128)S(1)}, s32[2,1536]{1,0:T(2,128)}, u32[]{:S(2)}) copy-start(s32[2,1536]{1,0:T(2,128)} %param.9) | copy-start | bytes 36868
  7.2 159.3 %copy-start.4 = (bf16[2,1536,512]{2,1,0:T(8,128)(2,1)S(1)}, bf16[2,1536,512]{2,1,0:T(8,128)(2,1)}, u32[]{:S(2)}) copy-start(bf16[2,1536,512]{2,1,0:T(8,128)(2,1)} %param.8) | copy-start | bytes 9437188
  7.2 159.3 %all-gather.7.cloned.1.call-start = ((), (), s32[]{:S(2)}) async-start(), calls=%async_computation.10 | async-start | bytes 14155776 | tf_op jit(solution)/shard_map/all_gather | solution.py:65
  11.2 307.8 %all-gather.5.cloned.1.call-start = ((), (), s32[]{:S(2)}) async-start(), calls=%async_computation.9 | async-start | bytes 14155776 | tf_op jit(solution)/shard_map/all_gather | solution.py:65
  12.6 11.6 %all-to-all-start = ((s32[16,1,256]{2,1,0:T(1,128)}), s32[16,1,256]{2,1,0:T(1,128)S(1)}, u32[]{:S(2)}, u32[]{:S(2)}) async-start(s32[16,1,256]{2,1,0:T(1,128)} %broadcast_in_dim.2), calls=%async_computation | async-start | bytes 32768 | tf_op jit(solution)/shard_map/all_to_all | solution.py:18
  18.1 397.2 %reduce-scatter.5.cloned.1.call-start = ((), (), s32[]{:S(2)}) async-start(), calls=%async_computation.8 | async-start | bytes 8912896 | tf_op jit(solution)/shard_map/reduce_scatter | solution.py:78
  220.5 296.8 %reduce-scatter.3.cloned.1.call-start = ((), (), s32[]{:S(2)}) async-start(), calls=%async_computation.7 | async-start | bytes 8912896 | tf_op jit(solution)/shard_map/reduce_scatter | solution.py:78
  373.5 0.7 copy-start.1
  419.7 102.0 %all-to-all-start.3 = ((f32[8,32,512]{2,1,0:T(8,128)}), f32[8,32,512]{2,1,0:T(8,128)S(1)}, u32[]{:S(2)}, u32[]{:S(2)}) async-start(f32[8,32,512]{2,1,0:T(8,128)} %bitcast.16), calls=%async_computation.5 | async-start | bytes 1048576 | tf_op jit(solution)/shard_map/all_to_all | solution.py:88
  424.6 134.6 %copy-start.2 = (s32[2]{0:T(128)S(1)}, s32[2]{0:T(128)}, u32[]{:S(2)}) copy-start(s32[2]{0:T(128)} %param.13) | copy-start | bytes 28
  521.6 18.5 %all-to-all-start.1 = ((f32[8,32,512]{2,1,0:T(8,128)}), f32[8,32,512]{2,1,0:T(8,128)S(1)}, u32[]{:S(2)}, u32[]{:S(2)}) async-start(f32[8,32,512]{2,1,0:T(8,128)} %bitcast.9), calls=%async_computation.2 | async-start | bytes 1048576 | tf_op jit(solution)/shard_map/all_to_all | solution.py:88
  540.1 15.5 %all-to-all-start.4 = ((f32[8,32,512]{2,1,0:T(8,128)}), f32[8,32,512]{2,1,0:T(8,128)S(1)}, u32[]{:S(2)}, u32[]{:S(2)}) async-start(f32[8,32,512]{2,1,0:T(8,128)} %copy.26), calls=%async_computation.6 | async-start | bytes 1048576 | tf_op jit(solution)/shard_map/all_to_all | solution.py:90
  555.6 14.5 %all-to-all-start.2 = ((f32[8,32,512]{2,1,0:T(8,128)}), f32[8,32,512]{2,1,0:T(8,128)S(1)}, u32[]{:S(2)}, u32[]{:S(2)}) async-start(f32[8,32,512]{2,1,0:T(8,128)} %copy.22), calls=%async_computation.3 | async-start | bytes 1048576 | tf_op jit(solution)/shard_map/all_to_all | solution.py:90
Sparse Core Ops, SparseCore 0:
  11.4 155.1 all-gather.6
  168.7 150.3 all-gather.4
  321.5 93.8 reduce-scatter.4
  417.6 99.6 reduce-scatter.2
where the time goes:
time: 628 us; the launch traced here: 618 us
  waiting for transfers between devices  406 us (65%)
  matrix products  73.7 us (12%)
  local copies, waits for them, and re-layouts  53 us (8%)
  blocking collectives  32.5 us (5%)
  starting transfers between devices  25.6 us (4%)
  between operations  18 us (3%)
  other arithmetic  9.12 us (1%)
    all_gather x2, waiting for transfers between devices, body(): features = lax.all_gather(activations[seq_number], COL, axis=1, tiled=True)  241 us
    reduce_scatter x2, waiting for transfers between devices, body(): lax.psum_scatter(term_rows(jnp.int32(0), lax.axis_size(TOK) * local_rows)...  134 us
    psum x5, blocking collectives, one_axis_at_a_time(): return functools.reduce(lax.psum, axes, x)  32.5 us
    dot_general x2, matrix products, body(): blocks = jnp.einsum('ab,brc->arc', tok_table, blocks, precision=HIGH)  23.4 us
    transpose x2, local copies, waits for them, and re-layouts, body(): blocks = jnp.einsum('rs,asc->arc', rows_table, blocks, precision=HIGH)  21 us
    dot_general x2, matrix products, body(): jnp.einsum('tr,tc->rc', features, masked, preferred_element_type=jnp.floa...  20.9 us
    dot_general x2, matrix products, body(): blocks = jnp.einsum('rs,asc->arc', rows_table, blocks, precision=HIGH)  19.2 us
    dot_general x2, local copies, waits for them, and re-layouts, body(): blocks = jnp.einsum('ab,brc->arc', tok_table, blocks, precision=HIGH)  16.1 us
  transfers between devices with their start and end apart: 9, of which 8 were waited for; matrix products, arithmetic and copies ran while one was open for 20% of the time, Pallas kernels for 0%

commit v1 on v0

--- a/solution.py
+++ b/solution.py
@@ -5,6 +5,7 @@
 from jax import lax
 from jax.sharding import Mesh
 from jax.sharding import PartitionSpec as P
+from jax.lax import all_to_all, axis_size
 
 D = 4096
 TOK = ("tok_0", "tok_1", "tok_2")
@@ -62,7 +63,10 @@
     owns = []
     refsqs = []
     for seq_number in range(activations.shape[0]):
-        features = lax.all_gather(activations[seq_number], COL, axis=1, tiled=True)
+        mine_x = activations[seq_number]
+        features = jnp.concatenate(
+            all_to_all(jnp.stack([mine_x] * axis_size(COL), 0), COL, split_axis=0, concat_axis=0), 1
+        )
         masked = out_grads[seq_number] * token_mask[seq_number][:, None].astype(jnp.bfloat16)
         partial_value = jnp.einsum(
             "tr,tc->rc", features, masked, preferred_element_type=jnp.float32

time: 628 us -> 725 us (1.15)
  blocking collectives: 32.5 us -> 258 us
  waiting for transfers between devices: 406 us -> 253 us
  local copies, waits for them, and re-layouts: 53 us -> 70.3 us
    all_gather x2 -> x0, waiting for transfers between devices: 241 us -> none  [body(): features = lax.all_gather(activations[seq_number], COL, axis=1, tiled=True)]
    all_to_all x0 -> x1, blocking collectives: none -> 225 us  [body(): all_to_all(jnp.stack([mine_x] * axis_size(COL), 0), COL, split_axis=0, co...]
    all_to_all x0 -> x1, waiting for transfers between devices: none -> 139 us  [body(): all_to_all(jnp.stack([mine_x] * axis_size(COL), 0), COL, split_axis=0, co...]
    reduce_scatter x2, waiting for transfers between devices: 134 us -> 88.5 us  [body(): lax.psum_scatter(term_rows(jnp.int32(0), lax.axis_size(TOK) * local_rows)...]
    another operation x0 -> x2, local copies, waits for them, and re-layouts: none -> 11.1 us  [body(): jnp.stack([mine_x] * axis_size(COL), 0)]
    all_to_all x0 -> x1, starting transfers between devices: none -> 7.78 us  [body(): all_to_all(jnp.stack([mine_x] * axis_size(COL), 0), COL, split_axis=0, co...]
  transfers between devices with their start and end apart: 9 -> 8, of which waited for: 8 -> 6; matrix products, arithmetic and copies ran while one was open for 20% -> 11% of each run, Pallas kernels for 0% -> 0%
where the time goes in v1:
time: 725 us; the launch traced here: 714 us
  blocking collectives  258 us (36%)
  waiting for transfers between devices  253 us (35%)
  matrix products  72.6 us (10%)
  local copies, waits for them, and re-layouts  70.3 us (10%)
  starting transfers between devices  32.6 us (4%)
  between operations  18.5 us (3%)
  other arithmetic  9.12 us (1%)
    all_to_all x1, blocking collectives, body(): all_to_all(jnp.stack([mine_x] * axis_size(COL), 0), COL, split_axis=0, co...  225 us
    all_to_all x1, waiting for transfers between devices, body(): all_to_all(jnp.stack([mine_x] * axis_size(COL), 0), COL, split_axis=0, co...  139 us
    reduce_scatter x2, waiting for transfers between devices, body(): lax.psum_scatter(term_rows(jnp.int32(0), lax.axis_size(TOK) * local_rows)...  88.5 us
    psum x5, blocking collectives, one_axis_at_a_time(): return functools.reduce(lax.psum, axes, x)  33 us
    dot_general x2, matrix products, body(): blocks = jnp.einsum('ab,brc->arc', tok_table, blocks, precision=HIGH)  22.9 us
    transpose x2, local copies, waits for them, and re-layouts, body(): blocks = jnp.einsum('rs,asc->arc', rows_table, blocks, precision=HIGH)  21.3 us
    dot_general x2, matrix products, body(): jnp.einsum('tr,tc->rc', features, masked, preferred_element_type=jnp.floa...  20.3 us
    dot_general x2, matrix products, body(): blocks = jnp.einsum('rs,asc->arc', rows_table, blocks, precision=HIGH)  19.2 us
  transfers between devices with their start and end apart: 8, of which 6 were waited for; matrix products, arithmetic and copies ran while one was open for 11% of the time, Pallas kernels for 0%

profile of v1, /device:TPU:0, one launch (start us, length us, event | category | flops | bytes accessed | tf_op | source)
XLA Modules:
  0.0 713.9 jit_solution(10503256583265065859)
XLA Ops:
  20.1 5.5 stack.39
  25.6 7.8 %all-to-all-start.4 = ((bf16[8,1536,512]{1,2,0:T(8,128)(2,1)}), bf16[8,1536,512]{1,2,0:T(8,128)(2,1)}, u32[]{:S(2)}, u32[]{:S(2)}) async-start(bf16[8,1536,512]{1,2,0:T(8,128)(2,1)} %stack.39), calls=%async_computation.5 | async-start | bytes 25165824 | tf_op jit(solution)/shard_map/all_to_all | solution.py:68
  33.6 139.0 %all-to-all-done.4 = bf16[8,1536,512]{1,2,0:T(8,128)(2,1)} async-done(((bf16[8,1536,512]{1,2,0:T(8,128)(2,1)}), bf16[8,1536,512]{1,2,0:T(8,128)(2,1)}, u32[]{:S(2)}, u32[]{:S(2)}) %all-to-all-start.4) | async-done | bytes 12582944 | tf_op jit(solution)/shard_map/all_to_all | solution.py:68
  172.6 10.8 %convolution_multiply_fusion = f32[512,4096]{1,0:T(8,128)S(1)} fusion(bf16[1536,4096]{0,1:T(8,128)(2,1)} %bitcast.16, f32[4096]{0:T(1024)S(1)} %bitcast.90, bf16[2,1536,512]{2,1,0:T(8,128)(2,1)} %param.8, bf16[1536]{0:T(1024)(128)(2,1)S(1)} %get-tuple-element.7), kind=kOutput, calls=%fused_computation | convolution fusion | flops 6445334528 | bytes 22563840 | tf_op jit(solution)/shard_map/tr,tc->rc/dot_general | solution.py:71
  187.3 9.6 %convolution_bitcast_fusion = f32[16,256,512]{1,0,2:T(8,128)} fusion(f32[16,256,512]{1,0,2:T(8,128)S(1)} %bitcast.83), kind=kOutput, calls=%fused_computation.2 | convolution fusion | flops 6444941312 | bytes 16777216 | tf_op jit(solution)/shard_map/rs,asc->arc/dot_general | solution.py:75
  196.9 10.8 %copy.27 = f32[16,256,512]{2,0,1:T(8,128)} copy(f32[16,256,512]{1,0,2:T(8,128)} %convolution_bitcast_fusion) | data formatting | bytes 16777216 | tf_op jit(solution)/shard_map/rs,asc->arc/transpose | solution.py:75
  207.7 11.4 %fusion.56 = f32[16,256,512]{2,0,1:T(8,128)S(1)} fusion(f32[16,256,512]{2,0,1:T(8,128)} %copy.27), kind=kOutput, calls=%fused_computation.77 | convolution fusion | flops 402659840 | bytes 16777216 | tf_op jit(solution)/shard_map/ab,brc->arc/dot_general | solution.py:76
  219.1 8.1 %copy.28 = f32[16,256,512]{2,1,0:T(8,128)} copy(f32[16,256,512]{2,0,1:T(8,128)S(1)} %fusion.56) | data formatting | bytes 16777216 | tf_op jit(solution)/shard_map/ab,brc->arc/dot_general | solution.py:76
  228.0 5.6 stack.38
  233.6 225.2 %all_to_all.36 = bf16[8,1536,512]{1,2,0:T(8,128)(2,1)S(1)} all-to-all(bf16[8,1536,512]{1,2,0:T(8,128)(2,1)} %stack.38), channel_id=1, replica_groups=mesh['tok_0'=4,'tok_1'=2,'tok_2'=2,'col_0'=2,'col_1'=4] {'col_0','col_1'}, dimensions={0} | all-to-all | bytes 25165824 | tf_op jit(solution)/shard_map/all_to_all | solution.py:68
  458.8 9.5 %convolution_multiply_fusion.1 = f32[512,4096]{1,0:T(8,128)} fusion(bf16[1536,4096]{0,1:T(8,128)(2,1)S(1)} %bitcast.85, f32[4096]{0:T(1024)S(1)} %bitcast.91, bf16[2,1536,512]{2,1,0:T(8,128)(2,1)S(1)} %copy-done.3, bf16[1536]{0:T(1024)(128)(2,1)S(1)} %get-tuple-element.6), kind=kOutput, calls=%fused_computation.1 | convolution fusion | flops 6445334528 | bytes 22564864 | tf_op jit(solution)/shard_map/tr,tc->rc/dot_general | solution.py:71
  468.3 7.3 %copy.31 = f32[64,8,16,256]{3,2,1,0:T(8,128)S(1)} copy(f32[64,8,16,256]{3,1,2,0:T(8,128)} %bitcast.86) | data formatting | bytes 16777216
  475.6 9.6 %convolution_bitcast_fusion.1 = f32[16,256,512]{1,0,2:T(8,128)} fusion(f32[16,256,512]{1,0,2:T(8,128)S(1)} %bitcast.84), kind=kOutput, calls=%fused_computation.3 | convolution fusion | flops 6444941312 | bytes 16777216 | tf_op jit(solution)/shard_map/rs,asc->arc/dot_general | solution.py:75
  485.1 10.5 %copy.22 = f32[16,256,512]{2,0,1:T(8,128)} copy(f32[16,256,512]{1,0,2:T(8,128)} %convolution_bitcast_fusion.1) | data formatting | bytes 16777216 | tf_op jit(solution)/shard_map/rs,asc->arc/transpose | solution.py:75
  495.6 11.6 %fusion.58 = f32[16,256,512]{2,0,1:T(8,128)S(1)} fusion(f32[16,256,512]{2,0,1:T(8,128)} %copy.22), kind=kOutput, calls=%fused_computation.78 | convolution fusion | flops 402659840 | bytes 16777216 | tf_op jit(solution)/shard_map/ab,brc->arc/dot_general | solution.py:76
  507.2 8.2 %copy.23 = f32[16,256,512]{2,1,0:T(8,128)} copy(f32[16,256,512]{2,0,1:T(8,128)S(1)} %fusion.58) | data formatting | bytes 16777216 | tf_op jit(solution)/shard_map/ab,brc->arc/dot_general | solution.py:76
  524.1 88.5 %reduce-scatter.3.cloned.1.call-done = f32[256,512]{1,0:T(8,128)} async-done(((f32[4096,512]{1,0:T(8,128)}), f32[256,512]{1,0:T(8,128)}) %reduce-scatter.3.cloned.1.call-update) | async-done | bytes 524304 | tf_op jit(solution)/shard_map/reduce_scatter | solution.py:82
  616.9 7.0 all-to-all-start.2
  625.8 8.7 %all-to-all-done.2 = f32[8,32,512]{2,1,0:T(8,128)S(1)} async-done(((f32[8,32,512]{2,1,0:T(8,128)}), f32[8,32,512]{2,1,0:T(8,128)S(1)}, u32[]{:S(2)}, u32[]{:S(2)}) %all-to-all-start.2) | async-done | bytes 524320 | tf_op jit(solution)/shard_map/all_to_all | solution.py:92
  641.5 9.3 %all-to-all-done.6 = f32[8,32,512]{2,1,0:T(8,128)S(1)} async-done(((f32[8,32,512]{2,1,0:T(8,128)}), f32[8,32,512]{2,1,0:T(8,128)S(1)}, u32[]{:S(2)}, u32[]{:S(2)}) %all-to-all-start.6) | async-done | bytes 524320 | tf_op jit(solution)/shard_map/all_to_all | solution.py:94
  659.5 5.7 all-to-all-done.3
  673.1 10.2 %all-reduce.1 = (f32[2]{0:T(128)S(1)}, f32[2]{0:T(128)S(1)}, f32[2]{0:T(128)S(1)}) all-reduce(f32[2]{0:T(128)S(1)} %pad_maximum_fusion.3, f32[2]{0:T(128)S(1)} %get-tuple-element.32, f32[2]{0:T(128)S(1)} %get-tuple-element.31), channel_id=1, replica_groups=mesh['tok_0'=4,'tok_1'=2,'tok_2'=2,'col_0'=2,'col_1'=4] {'tok_0'}, use_global_device_ids=true, to_apply=%region_18.19 | all-reduce | flops 6 | bytes 48 | tf_op jit(solution)/shard_map/psum | solution.py:34
  690.7 6.4 all-reduce.2
  697.1 9.0 %all-reduce = (f32[2]{0:T(128)S(1)}, f32[2]{0:T(128)S(1)}, f32[2]{0:T(128)S(1)}) all-reduce(f32[2]{0:T(128)S(1)} %get-tuple-element.14, f32[2]{0:T(128)S(1)} %get-tuple-element.15, f32[2]{0:T(128)S(1)} %get-tuple-element.16), channel_id=1, replica_groups=mesh['tok_0'=4,'tok_1'=2,'tok_2'=2,'col_0'=2,'col_1'=4] {'col_1'}, use_global_device_ids=true, to_apply=%region_22.23 | all-reduce | flops 6 | bytes 48 | tf_op jit(solution)/shard_map/psum | solution.py:34
  (44 shorter events, 60.0 us)
Async XLA Ops:
  8.5 11.6 %all-to-all-start.1 = ((s32[16,1,256]{2,1,0:T(1,128)}), s32[16,1,256]{2,1,0:T(1,128)S(1)}, u32[]{:S(2)}, u32[]{:S(2)}) async-start(s32[16,1,256]{2,1,0:T(1,128)} %broadcast_in_dim.2), calls=%async_computation.1 | async-start | bytes 32768 | tf_op jit(solution)/shard_map/all_to_all | solution.py:19
  25.6 7.8 %copy-start = (s32[2,1536]{1,0:T(2,128)S(1)}, s32[2,1536]{1,0:T(2,128)}, u32[]{:S(2)}) copy-start(s32[2,1536]{1,0:T(2,128)} %param.9) | copy-start | bytes 36868
  25.6 146.9 %all-to-all-start.4 = ((bf16[8,1536,512]{1,2,0:T(8,128)(2,1)}), bf16[8,1536,512]{1,2,0:T(8,128)(2,1)}, u32[]{:S(2)}, u32[]{:S(2)}) async-start(bf16[8,1536,512]{1,2,0:T(8,128)(2,1)} %stack.39), calls=%async_computation.5 | async-start | bytes 25165824 | tf_op jit(solution)/shard_map/all_to_all | solution.py:68
  33.4 482.6 %reduce-scatter.5.cloned.1.call-start = ((), (), s32[]{:S(2)}) async-start(), calls=%async_computation.10 | async-start | bytes 8912896 | tf_op jit(solution)/shard_map/reduce_scatter | solution.py:82
  227.2 385.4 %reduce-scatter.3.cloned.1.call-start = ((), (), s32[]{:S(2)}) async-start(), calls=%async_computation.9 | async-start | bytes 8912896 | tf_op jit(solution)/shard_map/reduce_scatter | solution.py:82
  233.5 225.2 %copy-start.3 = (bf16[2,1536,512]{2,1,0:T(8,128)(2,1)S(1)}, bf16[2,1536,512]{2,1,0:T(8,128)(2,1)}, u32[]{:S(2)}) copy-start(bf16[2,1536,512]{2,1,0:T(8,128)(2,1)} %param.8) | copy-start | bytes 9437188
  515.4 0.7 copy-start.1
  520.4 96.6 %all-to-all-start.5 = ((f32[8,32,512]{2,1,0:T(8,128)}), f32[8,32,512]{2,1,0:T(8,128)S(1)}, u32[]{:S(2)}, u32[]{:S(2)}) async-start(f32[8,32,512]{2,1,0:T(8,128)} %bitcast.20), calls=%async_computation.7 | async-start | bytes 1048576 | tf_op jit(solution)/shard_map/all_to_all | solution.py:92
  524.1 130.2 %copy-start.2 = (s32[2]{0:T(128)S(1)}, s32[2]{0:T(128)}, u32[]{:S(2)}) copy-start(s32[2]{0:T(128)} %param.13) | copy-start | bytes 28
  616.9 17.6 %all-to-all-start.2 = ((f32[8,32,512]{2,1,0:T(8,128)}), f32[8,32,512]{2,1,0:T(8,128)S(1)}, u32[]{:S(2)}, u32[]{:S(2)}) async-start(f32[8,32,512]{2,1,0:T(8,128)} %bitcast.11), calls=%async_computation.3 | async-start | bytes 1048576 | tf_op jit(solution)/shard_map/all_to_all | solution.py:92
  634.6 16.2 %all-to-all-start.6 = ((f32[8,32,512]{2,1,0:T(8,128)}), f32[8,32,512]{2,1,0:T(8,128)S(1)}, u32[]{:S(2)}, u32[]{:S(2)}) async-start(f32[8,32,512]{2,1,0:T(8,128)} %copy.30), calls=%async_computation.8 | async-start | bytes 1048576 | tf_op jit(solution)/shard_map/all_to_all | solution.py:94
  650.8 14.5 %all-to-all-start.3 = ((f32[8,32,512]{2,1,0:T(8,128)}), f32[8,32,512]{2,1,0:T(8,128)S(1)}, u32[]{:S(2)}, u32[]{:S(2)}) async-start(f32[8,32,512]{2,1,0:T(8,128)} %copy.25), calls=%async_computation.4 | async-start | bytes 1048576 | tf_op jit(solution)/shard_map/all_to_all | solution.py:94
Sparse Core Ops, SparseCore 0:
  227.3 167.9 reduce-scatter.4
  515.5 97.0 reduce-scatter.2
